TPU v7x, 256 devices: a whole 4x4x8 slice. The times are simulated.
256 devices in a mesh: prow: 16 (over y, x), pcol: 16 (over z, core).
Axes of the slice: x: 4, y: 4, z: 8, core: 2. Of those that a mesh axis runs over, the one named last changes fastest.
Arguments:
- blocked: float32 [16384, 16384], P('prow', 'pcol'), may hold values from -6 to 6, as said below
Outputs:
- factored: float32 [16384, 16384], P('prow', 'pcol')
Inputs may be any that keep to these rules, and one draw needn't show every extreme that they name: blocked is the block-cyclic storage of a symmetric positive definite matrix whose diagonal is at least 1 plus a nonnegative Gram diagonal and whose condition number is below about 40.
All inputs are finite; a program needn't handle non-finite values.
Results may differ from a plain program's by a relative error of at most 0.0003.
Values sent between devices are 32-bit elements.
A program may use at most 128 MiB of HBM per device.

v0:
```python
import jax
import jax.numpy as jnp
from jax import lax
from jax.sharding import PartitionSpec as P

BLOCK = 128
STEPS = 8


def broadcast(value, axis, source):
    kept = jnp.where(lax.axis_index(axis) == source, value, 0).astype(value.dtype)
    return lax.psum(kept, axis)


def per_device(blocked):
    local_rows, local_cols = blocked.shape
    prow_size = lax.axis_size("prow")
    pcol_size = lax.axis_size("pcol")
    row_index = lax.axis_index("prow")
    col_index = lax.axis_index("pcol")
    col_blocks = local_cols // BLOCK
    ratio = pcol_size // prow_size
    source_row = col_index % prow_size
    source_offset = col_index // prow_size
    row_global = jnp.arange(local_rows, dtype=jnp.int32) // BLOCK * prow_size + row_index
    col_global = jnp.arange(local_cols, dtype=jnp.int32) // BLOCK * pcol_size + col_index
    cleared = (row_global < STEPS)[:, None] & (col_global >= STEPS)[None, :]
    width = STEPS * BLOCK
    lead_cols = (STEPS + pcol_size - 1) // pcol_size
    lead_rows = (STEPS + prow_size - 1) // prow_size
    gathered = lax.all_gather(blocked[:, : lead_cols * BLOCK], "pcol", axis=1, tiled=True)
    gathered = gathered.reshape(local_rows, pcol_size, lead_cols, BLOCK).transpose(0, 2, 1, 3)
    gathered = gathered.reshape(local_rows, pcol_size * lead_cols * BLOCK)
    strip = gathered[:, :width]
    window = lax.all_gather(strip[: lead_rows * BLOCK], "prow", axis=0, tiled=True)
    window = window.reshape(prow_size, lead_rows, BLOCK, width).transpose(1, 0, 2, 3)
    window = window.reshape(prow_size * lead_rows * BLOCK, width)[:width]
    leading = jnp.tril(jnp.linalg.cholesky(window))
    solved = jax.scipy.linalg.solve_triangular(leading, strip.T, lower=True).T
    outside = (row_global >= STEPS)[:, None]
    rows = jnp.where(outside, solved, 0.0)
    picked = lax.dynamic_index_in_dim(
        rows.reshape(col_blocks, ratio, BLOCK, width), source_offset, 1, keepdims=False
    )
    columns = broadcast(picked.reshape(local_cols, width), "prow", source_row)
    matrix = blocked - jnp.dot(rows, columns.T, precision=lax.Precision.HIGHEST)
    natural_row = row_global * BLOCK + jnp.arange(local_rows, dtype=jnp.int32) % BLOCK
    natural_row = jnp.minimum(natural_row, width - 1).astype(jnp.int32)
    new_strip = jnp.where(outside, solved, leading[natural_row])
    padded = jnp.pad(new_strip, ((0, 0), (0, pcol_size * lead_cols * BLOCK - width)))
    padded = padded.reshape(local_rows, lead_cols, pcol_size, BLOCK)
    mine = lax.dynamic_index_in_dim(padded, col_index, 2, keepdims=False).reshape(
        local_rows, lead_cols * BLOCK
    )
    inside = (col_global[: lead_cols * BLOCK] < STEPS)[None, :]
    head = jnp.where(inside, mine, matrix[:, : lead_cols * BLOCK])
    matrix = matrix.at[:, : lead_cols * BLOCK].set(head)
    return jnp.where(cleared, 0.0, matrix)


def solution(mesh):
    return jax.shard_map(
        per_device,
        mesh=mesh,
        in_specs=(P("prow", "pcol"),),
        out_specs=P("prow", "pcol"),
        check_vma=False,
    )
```

profile of v0, /device:TPU:2, one launch (start us, length us, event | category | flops | bytes accessed | tf_op | source)
XLA Modules:
  0.0 688.9 jit_solution(3740926877962170286)
XLA Ops:
  8.7 59.2 %all-gather.3.cloned.1.call-done = f32[1024,2048]{0,1:T(8,128)} async-done(((f32[1024,128]{0,1:T(8,128)}), f32[1024,2048]{0,1:T(8,128)}) %all-gather.3.cloned.1.call-update) | async-done | bytes 8388624 | tf_op jit(solution)/shard_map/all_gather | solution.py:31
  74.6 75.4 %all-gather.5.cloned.1.call-done = f32[2048,1024]{0,1:T(8,128)} async-done(((f32[128,1024]{0,1:T(8,128)}), f32[2048,1024]{0,1:T(8,128)}) %all-gather.5.cloned.1.call-update) | async-done | bytes 8388624 | tf_op jit(solution)/shard_map/all_gather | solution.py:35
  166.5 11.7 %cholesky.222 = f32[128,128]{1,0:T(8,128)S(1)} custom-call(f32[128,128]{1,0:T(8,128)S(1)} %cholesky.577), custom_call_target="Cholesky" | custom-call | tf_op jit(solution)/shard_map/jit(cholesky)/cholesky | solution.py:38
  178.2 9.8 %custom-call.63 = f32[1,128,128]{1,2,0:T(8,128)S(1)} custom-call(f32[1,128,128]{2,1,0:T(8,128)S(1)} %get-tuple-element.77), custom_call_target="InvertDiagBlocksLowerTriangular" | custom-call | tf_op jit(solution)/shard_map/jit(cholesky)/cholesky | solution.py:38
  194.5 12.0 %cholesky.243 = f32[128,128]{1,0:T(8,128)S(1)} custom-call(f32[128,128]{1,0:T(8,128)S(1)} %cholesky.581), custom_call_target="Cholesky" | custom-call | tf_op jit(solution)/shard_map/jit(cholesky)/cholesky | solution.py:38
  207.1 9.8 %custom-call.64 = f32[1,128,128]{1,2,0:T(8,128)S(1)} custom-call(f32[1,128,128]{2,1,0:T(8,128)S(1)} %get-tuple-element.74), custom_call_target="InvertDiagBlocksLowerTriangular" | custom-call | tf_op jit(solution)/shard_map/jit(cholesky)/cholesky | solution.py:38
  220.3 11.7 %cholesky.466 = f32[128,128]{1,0:T(8,128)S(1)} custom-call(f32[128,128]{1,0:T(8,128)S(1)} %cholesky.586), custom_call_target="Cholesky" | custom-call | tf_op jit(solution)/shard_map/jit(cholesky)/cholesky | solution.py:38
  233.3 9.8 %custom-call.65 = f32[1,128,128]{1,2,0:T(8,128)S(1)} custom-call(f32[1,128,128]{2,1,0:T(8,128)S(1)} %get-tuple-element.71), custom_call_target="InvertDiagBlocksLowerTriangular" | custom-call | tf_op jit(solution)/shard_map/jit(cholesky)/cholesky | solution.py:38
  246.6 11.8 %cholesky.485 = f32[128,128]{1,0:T(8,128)S(1)} custom-call(f32[128,128]{1,0:T(8,128)S(1)} %cholesky.591), custom_call_target="Cholesky" | custom-call | tf_op jit(solution)/shard_map/jit(cholesky)/cholesky | solution.py:38
  259.8 9.8 %custom-call.66 = f32[1,128,128]{1,2,0:T(8,128)S(1)} custom-call(f32[1,128,128]{2,1,0:T(8,128)S(1)} %get-tuple-element.68), custom_call_target="InvertDiagBlocksLowerTriangular" | custom-call | tf_op jit(solution)/shard_map/jit(cholesky)/cholesky | solution.py:38
  273.0 11.7 %cholesky.504 = f32[128,128]{1,0:T(8,128)S(1)} custom-call(f32[128,128]{1,0:T(8,128)S(1)} %cholesky.596), custom_call_target="Cholesky" | custom-call | tf_op jit(solution)/shard_map/jit(cholesky)/cholesky | solution.py:38
  286.0 10.0 %custom-call.67 = f32[1,128,128]{1,2,0:T(8,128)S(1)} custom-call(f32[1,128,128]{2,1,0:T(8,128)S(1)} %get-tuple-element.65), custom_call_target="InvertDiagBlocksLowerTriangular" | custom-call | tf_op jit(solution)/shard_map/jit(cholesky)/cholesky | solution.py:38
  299.3 11.7 %cholesky.524 = f32[128,128]{1,0:T(8,128)S(1)} custom-call(f32[128,128]{1,0:T(8,128)S(1)} %cholesky.601), custom_call_target="Cholesky" | custom-call | tf_op jit(solution)/shard_map/jit(cholesky)/cholesky | solution.py:38
  312.3 9.8 %custom-call.68 = f32[1,128,128]{1,2,0:T(8,128)S(1)} custom-call(f32[1,128,128]{2,1,0:T(8,128)S(1)} %get-tuple-element.62), custom_call_target="InvertDiagBlocksLowerTriangular" | custom-call | tf_op jit(solution)/shard_map/jit(cholesky)/cholesky | solution.py:38
  325.2 12.1 %cholesky.544 = f32[128,128]{1,0:T(8,128)S(1)} custom-call(f32[128,128]{1,0:T(8,128)S(1)} %cholesky.606), custom_call_target="Cholesky" | custom-call | tf_op jit(solution)/shard_map/jit(cholesky)/cholesky | solution.py:38
  338.5 9.8 %custom-call.69 = f32[1,128,128]{1,2,0:T(8,128)S(1)} custom-call(f32[1,128,128]{2,1,0:T(8,128)S(1)} %get-tuple-element.59), custom_call_target="InvertDiagBlocksLowerTriangular" | custom-call | tf_op jit(solution)/shard_map/jit(cholesky)/cholesky | solution.py:38
  351.0 11.7 %cholesky.562 = f32[128,128]{1,0:T(8,128)S(1)} custom-call(f32[128,128]{1,0:T(8,128)S(1)} %convolution_subtract_fusion.11), custom_call_target="Cholesky" | custom-call | tf_op jit(solution)/shard_map/jit(cholesky)/cholesky | solution.py:38
  369.6 6.8 fusion.1
  376.4 22.8 %while.2 = (s32[]{:T(128)}, f32[1024,1024]{1,0:T(8,128)}, s32[8,2]{0,1:T(2,128)S(1)}, f32[8,128,128]{2,1,0:T(8,128)S(1)}, s32[]{:T(128)}) while((s32[]{:T(128)}, f32[1024,1024]{1,0:T(8,128)}, s32[8,2]{0,1:T(2,128)S(1)}, f32[8,128,128]{2,1,0:T(8,128)S(1)}, s32[]{:T(128)}) %tuple.60), condition=%wide.while_cond.1, body=%wide.while_body.1.sunk | while | flops 2 | bytes 131181 | solution.py:39
  399.3 78.8 %custom-call.70 = f32[8,128,128]{1,2,0:T(8,128)S(1)} custom-call(f32[8,128,128]{2,1,0:T(8,128)S(1)} %get-tuple-element.24), custom_call_target="InvertDiagBlocksLowerTriangular" | custom-call | tf_op jit(solution)/shard_map/jit(_solve_triangular)/triangular_solve | solution.py:39
  531.0 8.5 %gather_fusion = f32[1024,1024]{1,0:T(8,128)} fusion(f32[1024,1024]{1,0:T(8,128)} %get-tuple-element.34, s32[1024]{0:T(1024)S(1)} %broadcast_clamp_fusion), kind=kCustom, calls=%fused_computation | custom fusion | bytes 8392704 | tf_op jit(solution)/shard_map/gather | solution.py:49
  539.5 7.4 %bitcast_select_fusion = (f32[1024,1024]{1,0:T(8,128)}, f32[1024,1024]{1,0:T(8,128)}) fusion(f32[1024,1024]{1,0:T(8,128)} %gather_fusion, f32[1024,1024]{0,1:T(8,128)} %convolution_dynamic-update-slice_fusion, pred[1024]{0:T(1024)(128)(4,1)S(1)} %fusion.80, pred[]{:T(512)S(6)} %eq.7), kind=kLoop, calls=%fused_computation.6 | loop fusion | flops 3145728 | bytes 16778240 | tf_op jit(solution)/shard_map/jit(_where)/select_n | solution.py:49
  553.1 107.3 %all-reduce.4.cloned.1.call-done = f32[1024,1024]{1,0:T(8,128)} async-done(((f32[1024,1024]{1,0:T(8,128)}), f32[1024,1024]{1,0:T(8,128)}) %all-reduce.4.cloned.1.call-update) | async-done | bytes 4194320 | tf_op jit(solution)/shard_map/psum | solution.py:12
  660.4 18.3 %fusion.14 = f32[1024,1024]{1,0:T(8,128)S(1)} fusion(f32[1024,1024]{1,0:T(8,128)} %param.3, f32[1024,1024]{1,0:T(8,128)} %all-reduce.4.cloned.1.call-done, f32[1024,1024]{0,1:T(8,128)} %convolution_dynamic-update-slice_fusion, pred[1024]{0:T(1024)(128)(4,1)S(1)} %fusion.80), kind=kOutput, calls=%fused_computation.25 | convolution fusion | flops 12886999040 | bytes 16778240 | tf_op jit(solution)/shard_map/dot_general | solution.py:46
  (128 shorter events, 144.9 us)
Async XLA Ops:
  6.5 61.3 %all-gather.3.cloned.1.call-start = ((), (), s32[]{:S(2)}) async-start(), calls=%async_computation | async-start | bytes 8912896 | tf_op jit(solution)/shard_map/all_gather | solution.py:31
  8.6 141.4 %all-gather.5.cloned.1.call-start = ((), (), s32[]{:S(2)}) async-start(), calls=%async_computation.1 | async-start | bytes 8912896 | tf_op jit(solution)/shard_map/all_gather | solution.py:35
  69.8 590.6 %all-reduce.4.cloned.1.call-start = ((), (), s32[]{:S(2)}) async-start(), calls=%async_computation.2 | async-start | bytes 8388608 | tf_op jit(solution)/shard_map/psum | solution.py:12
  164.6 1.9 copy-start
  478.0 12.6 %copy-start.4 = (f32[8,128,128]{1,2,0:T(8,128)}, f32[8,128,128]{1,2,0:T(8,128)S(1)}, u32[]{:S(2)}) copy-start(f32[8,128,128]{1,2,0:T(8,128)S(1)} %custom-call.70) | copy-start | bytes 1572868
  518.0 9.5 %copy-start.1 = (f32[128,1024]{0,1:T(8,128)S(1)}, f32[128,1024]{0,1:T(8,128)}, u32[]{:S(2)}) copy-start(f32[128,1024]{0,1:T(8,128)} %copy.21) | copy-start | bytes 1572868
  522.2 3.5 copy-start.3
  522.2 4.4 copy-start.2
Sparse Core Ops, SparseCore 0:
  9.2 58.6 all-gather.2
  70.3 79.6 all-gather.4
  547.1 113.2 all-reduce.3
where the time goes:
time: 700 us; the launch traced here: 689 us
  other arithmetic  274 us (39%)
  waiting for transfers between devices  242 us (35%)
  matrix products  81.9 us (12%)
  local copies, waits for them, and re-layouts  72.1 us (10%)
  between operations  18.9 us (3%)
    another operation x30, other arithmetic, per_device(): leading = jnp.tril(jnp.linalg.cholesky(window))  173 us
    psum x1, waiting for transfers between devices, broadcast(): return lax.psum(kept, axis)  107 us
    another operation x3, other arithmetic, per_device(): solved = jax.scipy.linalg.solve_triangular(leading, strip.T, lower=True).T  85.6 us
    all_gather x1, waiting for transfers between devices, per_device(): lax.all_gather(strip[:lead_rows * BLOCK], 'prow', axis=0, tiled=True)  75.4 us
    all_gather x1, waiting for transfers between devices, per_device(): lax.all_gather(blocked[:, :lead_cols * BLOCK], 'pcol', axis=1, tiled=True)  59.2 us
    another operation x15, matrix products, per_device(): solved = jax.scipy.linalg.solve_triangular(leading, strip.T, lower=True).T  40.7 us
    another operation x14, matrix products, per_device(): leading = jnp.tril(jnp.linalg.cholesky(window))  22.9 us
    another operation x24, local copies, waits for them, and re-layouts  22.7 us
  transfers between devices with their start and end apart: 3, of which 3 were waited for; matrix products, arithmetic and copies ran while one was open for 2% of the time, Pallas kernels for 0%

commit v1 on v0

v1 whole, which is shorter than its diff:
```python
import functools

import jax
import jax.numpy as jnp
from jax import lax
from jax.experimental import pallas as pl
from jax.experimental.pallas import tpu as pltpu
from jax.sharding import PartitionSpec as P

BLOCK = 128
STEPS = 8
WIDTH = BLOCK * STEPS
TILE = 8
TILES = BLOCK // TILE
SIDE = 4
RING = 8
ZCHUNKS = 8
QCHUNKS = 4
ZROWS = WIDTH // ZCHUNKS
QROWS = BLOCK // QCHUNKS

UP = ((0, 1, 2), (1, 2, 3), (2, 3, 4, 5, 6, 7), (3, 4, 5, 6, 7, 0))
DOWN = ((0, 7, 6, 5, 4, 3), (1, 0, 7, 6, 5, 4), (2, 1, 0), (3, 2, 1))


def any_of(value, choices):
    hit = value == choices[0]
    for choice in choices[1:]:
        hit = hit | (value == choice)
    return hit


class Links:
    def __init__(self, ap, aq, wb, zsem, zsend, qsem, qsend, wsem, wsend):
        self.ap, self.aq, self.wb = ap, aq, wb
        self.zsem, self.zsend = zsem, zsend
        self.qsem, self.qsend = qsem, qsend
        self.wsem, self.wsend = wsem, wsend
        self.p, self.q = lax.axis_index("prow"), lax.axis_index("pcol")
        self.y, self.x = self.p // SIDE, self.p % SIDE
        self.z, self.c = self.q // 2, self.q % 2

    def device(self, dx=0, dy=0, dz=0, dc=0):
        prow = (self.y + dy) % SIDE * SIDE + (self.x + dx) % SIDE
        pcol = (self.z + dz) % RING * 2 + (self.c + dc) % 2
        return (prow, pcol)

    def neighbours(self):
        return [
            self.device(dx=1), self.device(dx=-1), self.device(dy=1), self.device(dy=-1),
            self.device(dz=1), self.device(dz=-1), self.device(dc=1),
        ]

    def copy(self, src, dst, send, recv, device):
        return pltpu.make_async_remote_copy(
            src_ref=src, dst_ref=dst, send_sem=send, recv_sem=recv,
            device_id=device, device_id_type=pl.DeviceIdType.MESH,
        )

    def zcopy(self, way, m, t, parity, device):
        j = 2 * m + parity
        part = self.ap.at[j, pl.ds(t * ZROWS, ZROWS)]
        return self.copy(part, part, self.zsend.at[way, m, t], self.zsem.at[j, t], device)

    def zstep(self, m, t):
        here = self.zcopy(0, m, t, self.c, self.device(dz=1))

        @pl.when(self.z != m)
        def _():
            here.wait_recv()

        @pl.when(any_of(self.z, UP[m][:-1]))
        def _():
            here.start()

        @pl.when(any_of(self.z, DOWN[m][:-1]))
        def _():
            self.zcopy(1, m, t, self.c, self.device(dz=-1)).start()

        self.zcopy(2, m, t, self.c, self.device(dc=1)).start()

    def ztwin(self, m, t):
        self.zcopy(2, m, t, 1 - self.c, self.device(dc=1)).wait_recv()

    def zdrain(self):
        for t in range(ZCHUNKS):
            for m in range(4):
                @pl.when(any_of(self.z, UP[m][:-1]))
                def _():
                    self.zcopy(0, m, t, self.c, self.device(dz=1)).wait_send()

                @pl.when(any_of(self.z, DOWN[m][:-1]))
                def _():
                    self.zcopy(1, m, t, self.c, self.device(dz=-1)).wait_send()

                self.zcopy(2, m, t, self.c, self.device(dc=1)).wait_send()

    def qcopy(self, way, i, t):
        device = (self.device(dy=1), self.device(dy=-1), self.device(dx=1), self.device(dx=-1))[way]
        part = self.aq.at[i, pl.ds(t * QROWS, QROWS)]
        return self.copy(part, part, self.qsend.at[way, i, t], self.qsem.at[i, t], device)

    def qways(self, i):
        ys, xs = i // SIDE, i % SIDE
        dx = (self.x - xs + SIDE) % SIDE
        same, own = dx == 0, self.y == ys
        if ys == 0:
            return (same & own, same & (own | (self.y == 3)), (dx == 0) | (dx == 1), dx == 0)
        return (same & (own | (self.y == 2)), same & own, dx == 0, (dx == 0) | (dx == 3))

    def qstep(self, i, t):
        @pl.when(self.p != i)
        def _():
            self.qcopy(0, i, t).wait_recv()

        for way, sends in enumerate(self.qways(i)):
            @pl.when(sends)
            def _():
                self.qcopy(way, i, t).start()

    def qdrain(self):
        for t in range(QCHUNKS):
            for i in range(STEPS):
                for way, sends in enumerate(self.qways(i)):
                    @pl.when(sends)
                    def _():
                        self.qcopy(way, i, t).wait_send()

    def wcopy(self, way, k, j, parity, own=False):
        device = (
            self.device(dy=1), self.device(dy=-1), self.device(dx=1), self.device(dx=-1), self.device(dc=1),
        )[way]
        dst = self.wb.at[k, j]
        src = self.ap.at[j, pl.ds(0, BLOCK)] if own else dst
        return self.copy(src, dst, self.wsend.at[way, k, j // 2], self.wsem.at[k, j], device)

    def wways(self, k):
        ys, xs = k // SIDE, k % SIDE
        dx = (self.x - xs + SIDE) % SIDE
        row = self.y == ys
        if ys == 0:
            return (row, row | (self.y == 3), row & ((dx == 0) | (dx == 1)), row & (dx == 0), self.p != k)
        return (row | (self.y == 2), row, row & (dx == 0), row & ((dx == 0) | (dx == 3)), self.p != k)

    def wstep(self, k, j):
        @pl.when(self.c == j % 2)
        def _():
            @pl.when(self.p != k)
            def _():
                self.wcopy(0, k, j, self.c).wait_recv()

            for way, sends in enumerate(self.wways(k)):
                @pl.when(sends & (self.p != k))
                def _():
                    self.wcopy(way, k, j, self.c).start()
                if way < 4:
                    @pl.when(sends & (self.p == k))
                    def _():
                        self.wcopy(way, k, j, self.c, own=True).start()

    def wtwin(self, k, j):
        @pl.when((self.c != j % 2) & (self.p != k))
        def _():
            self.wcopy(4, k, j, 1 - self.c).wait_recv()

    def wdrain(self):
        for k in range(STEPS):
            for j in range(k, STEPS):
                for way, sends in enumerate(self.wways(k)):
                    @pl.when(sends & (self.c == j % 2))
                    def _():
                        self.wcopy(way, k, j, self.c).wait_send()


def gather_kernel(t_ref, ap_out, aq_out, wb_out, ap, aq, wb, lsem, osem, *sems):
    net = Links(ap, aq, wb, *sems)
    barrier = pltpu.get_barrier_semaphore()
    for device in net.neighbours():
        pl.semaphore_signal(barrier, inc=1, device_id=device, device_id_type=pl.DeviceIdType.MESH)
    head = pltpu.make_async_copy(t_ref.at[pl.ds(0, BLOCK), pl.ds(0, BLOCK)], ap.at[net.q % STEPS, pl.ds(0, BLOCK)], lsem.at[0])
    body = pltpu.make_async_copy(
        t_ref.at[pl.ds(BLOCK, WIDTH - BLOCK), pl.ds(0, BLOCK)],
        ap.at[net.q % STEPS, pl.ds(BLOCK, WIDTH - BLOCK)], lsem.at[1],
    )
    rows = pltpu.make_async_copy(t_ref.at[pl.ds(0, BLOCK)], aq.at[net.p % STEPS], lsem.at[2])

    @pl.when(net.q < STEPS)
    def _():
        head.start()
        body.start()
        head.wait()
        body.wait()

    @pl.when(net.p < STEPS)
    def _():
        rows.start()
        rows.wait()

    pl.semaphore_wait(barrier, 7)
    for m in range(4):
        net.zstep(m, 0)
    for t in range(QCHUNKS):
        for i in range(STEPS):
            @pl.when(net.p == i)
            def _():
                net.qstep(i, t)
    for m in range(4):
        net.ztwin(m, 0)
    for k in range(STEPS):
        @pl.when(net.p == k)
        def _():
            for j in range(STEPS):
                wb[k, j] = ap[j, 0:BLOCK]
    for k in range(STEPS):
        for j in range(k, STEPS):
            net.wstep(k, j)
        if k:
            for m in range(4):
                net.zstep(m, k)
    for t in range(QCHUNKS):
        for i in range(STEPS):
            @pl.when(net.p != i)
            def _():
                net.qstep(i, t)
    for t in range(1, ZCHUNKS):
        for m in range(4):
            net.ztwin(m, t)
    for k in range(STEPS):
        for j in range(k, STEPS):
            net.wtwin(k, j)
    outs = [
        pltpu.make_async_copy(src, dst, osem.at[n])
        for n, (src, dst) in enumerate(((ap, ap_out), (aq, aq_out), (wb, wb_out)))
    ]
    for out in outs:
        out.start()
    net.zdrain()
    net.qdrain()
    net.wdrain()
    for out in outs:
        out.wait()


def row_of(x, j):
    return jnp.broadcast_to(x[j : j + 1, :], (TILE, BLOCK))


def lane_of(x, c):
    return jnp.broadcast_to(x[:, c : c + 1], x.shape)


def times(x, n):
    return x if n == 1 else jnp.concatenate([x] * n, axis=0)


def invert_factor(block):
    sub = lax.broadcasted_iota(jnp.int32, (TILE, BLOCK), 0)
    rows = lax.broadcasted_iota(jnp.int32, (BLOCK, BLOCK), 0)
    lanes = lax.broadcasted_iota(jnp.int32, (BLOCK, BLOCK), 1)
    ident = jnp.where(rows == lanes, 1.0, 0.0).astype(jnp.float32)
    head, rest = block[:TILE], block[TILE:]
    bhead, brest = ident[:TILE], ident[TILE:]
    done = []
    ahead = [lane_of(head, j) for j in range(TILE)]
    for s in range(TILES):
        left = TILES - 1 - s
        first = TILE * s
        col = ahead
        if left:
            below = [lane_of(rest, first + j) for j in range(TILE)]
            ahead = [lane_of(rest[:TILE], first + TILE + j) for j in range(TILE)]
        r, b = head, bhead
        scale, coef = [], {}
        for j in range(TILE):
            scale.append(lax.rsqrt(row_of(col[j], j)))
            line = col[j] * scale[j]
            for k in range(j + 1, TILE):
                coef[j, k] = row_of(line, k)
                col[k] = col[k] - line * coef[j, k]
            ru, bu = row_of(r, j) * scale[j], row_of(b, j) * scale[j]
            if j < TILE - 1:
                low = jnp.where(sub > j, line, 0.0)
                r = jnp.where(sub == j, ru, r - low * ru)
                b = jnp.where(sub == j, bu, b - low * bu)
            else:
                r = jnp.where(sub == j, ru, r)
                b = jnp.where(sub == j, bu, b)
        done.append(b)
        if not left:
            break
        lines = []
        for j in range(TILE):
            line = below[j] * times(scale[j], left)
            lines.append(line)
            for k in range(j + 1, TILE):
                below[k] = below[k] - line * times(coef[j, k], left)
        for m in range(TILE):
            near = lines[m][:TILE]
            for j in range(TILE):
                ahead[j] = ahead[j] - near * row_of(near, j)
        for j in range(TILE):
            rest = rest - lines[j] * times(row_of(r, j), left)
            brest = brest - lines[j] * times(row_of(b, j), left)
        head, rest = rest[:TILE], rest[TILE:]
        bhead, brest = brest[:TILE], brest[TILE:]
    return jnp.concatenate(done, axis=0)


def split(x):
    high = x.astype(jnp.bfloat16)
    return high, (x - high.astype(jnp.float32)).astype(jnp.bfloat16)


NN = (((1,), (0,)), ((), ()))
TN = (((0,), (0,)), ((), ()))
NT = (((1,), (1,)), ((), ()))


def dot3(a, b, dims):
    one = functools.partial(lax.dot_general, dimension_numbers=dims, preferred_element_type=jnp.float32)
    return one(a[0], b[0]) + one(a[0], b[1]) + one(a[1], b[0])


def update_kernel(t_ref, ap, aq, wb, out, lpf, uh, ul, xh, xl, aph, apl, aqh, aql, diag):
    p, q = lax.axis_index("prow"), lax.axis_index("pcol")
    xh[...] = jnp.zeros_like(xh)
    xl[...] = jnp.zeros_like(xl)
    for j in range(STEPS):
        aqh[j * BLOCK : (j + 1) * BLOCK, :], aql[j * BLOCK : (j + 1) * BLOCK, :] = split(aq[j])
        aph[:, j * BLOCK : (j + 1) * BLOCK], apl[:, j * BLOCK : (j + 1) * BLOCK] = split(ap[j])
    diag[...] = wb[0, 0]

    def step(k, carry):
        inv = invert_factor(diag[...])
        ih, il = split(inv)
        for kk in range(STEPS):
            lo, hi = kk * BLOCK, (kk + 1) * BLOCK

            @pl.when(k == kk)
            def _():
                xh[lo:hi, lo:hi] = ih
                xl[lo:hi, lo:hi] = il
                if kk:
                    lead = (uh[:lo, lo:hi], ul[:lo, lo:hi])
                    gx = split(dot3(lead, (xh[:lo, :lo], xl[:lo, :lo]), TN))
                    xrow = split(-dot3((ih, il), gx, NN))
                    xh[lo:hi, :lo], xl[lo:hi, :lo] = xrow
                if kk < STEPS - 1:
                    g = jnp.concatenate([wb[kk, j] for j in range(kk + 1, STEPS)], axis=1)
                    if kk:
                        g = g - dot3(lead, (uh[:lo, hi:], ul[:lo, hi:]), TN)
                    urow = split(dot3((ih, il), split(g), NN))
                    uh[lo:hi, hi:], ul[lo:hi, hi:] = urow
                    nxt = (uh[:hi, hi : hi + BLOCK], ul[:hi, hi : hi + BLOCK])
                    diag[...] = wb[kk + 1, kk + 1] - dot3(nxt, nxt, TN)

        return carry

    lax.fori_loop(0, STEPS, step, 0)
    lqh, lql = uh, ul
    wide = 2 * BLOCK
    for b in range(STEPS // 2):
        end = wide * (b + 1)
        rows = pl.ds(wide * b, wide)
        xb = (xh[rows, :end], xl[rows, :end])
        lqh[rows, :], lql[rows, :] = split(dot3(xb, (aqh[:end, :], aql[:end, :]), NN))

        def part(i, carry, b=b, end=end, xb=xb, rows=rows):
            mine = pl.ds(pl.multiple_of(i * wide, wide), wide)
            lp = dot3((aph[mine, :end], apl[mine, :end]), xb, NT)
            lpf[2 * b, mine] = lp[:, :BLOCK]
            lpf[2 * b + 1, mine] = lp[:, BLOCK:]
            prev = t_ref[mine, :] if b == 0 else out[mine, :]
            out[mine, :] = prev - dot3(split(lp), (lqh[rows, :], lql[rows, :]), NN)
            return carry

        lax.fori_loop(0, WIDTH // wide, part, 0)

    @pl.when(p < STEPS)
    def _():
        out[0:BLOCK, :] = jnp.zeros((BLOCK, WIDTH), jnp.float32)

    @pl.when(q < STEPS)
    def _():
        out[BLOCK:, 0:BLOCK] = lpf[q % STEPS, BLOCK:]
        top = lpf[q % STEPS, 0:BLOCK]
        rows = lax.broadcasted_iota(jnp.int32, (BLOCK, BLOCK), 0) + p * BLOCK
        lanes = lax.broadcasted_iota(jnp.int32, (BLOCK, BLOCK), 1) + q * BLOCK
        out[0:BLOCK, 0:BLOCK] = jnp.where((p >= STEPS) | (rows >= lanes), top, 0.0)


def per_device(blocked):
    f32, bf16 = jnp.float32, jnp.bfloat16
    hbm = pl.BlockSpec(memory_space=pl.ANY)
    slabs = [(STEPS, WIDTH, BLOCK), (STEPS, BLOCK, WIDTH), (STEPS, STEPS, BLOCK, BLOCK)]
    dma = pltpu.SemaphoreType.DMA
    ap, aq, wb = pl.pallas_call(
        gather_kernel,
        name="gather",
        out_shape=[jax.ShapeDtypeStruct(s, f32) for s in slabs],
        in_specs=[hbm],
        out_specs=[hbm] * 3,
        scratch_shapes=[
            *(pltpu.VMEM(s, f32) for s in slabs),
            dma((3,)), dma((3,)),
            dma((8, ZCHUNKS)), dma((3, 4, ZCHUNKS)),
            dma((8, QCHUNKS)), dma((4, 8, QCHUNKS)),
            dma((8, 8)), dma((5, 8, 4)),
        ],
        compiler_params=pltpu.CompilerParams(collective_id=0, has_side_effects=True, vmem_limit_bytes=40 << 20),
    )(blocked)
    vmem = pl.BlockSpec(memory_space=pltpu.VMEM)
    square = (WIDTH, WIDTH)
    return pl.pallas_call(
        update_kernel,
        name="update",
        out_shape=jax.ShapeDtypeStruct(square, f32),
        in_specs=[vmem] * 4,
        out_specs=vmem,
        scratch_shapes=[
            pltpu.VMEM(slabs[0], f32),
            *(pltpu.VMEM(square, bf16) for _ in range(8)),
            pltpu.VMEM((BLOCK, BLOCK), f32),
        ],
        compiler_params=pltpu.CompilerParams(vmem_limit_bytes=60 << 20),
    )(blocked, ap, aq, wb)


def solution(mesh):
    return jax.shard_map(
        per_device,
        mesh=mesh,
        in_specs=(P("prow", "pcol"),),
        out_specs=P("prow", "pcol"),
        check_vma=False,
    )
```

time: 700 us -> 626 us (0.89)
  the two profiles are of different devices: /device:TPU:2 before, /device:TPU:26 now
where the time goes in v1:
time: 626 us
  Pallas kernels  620 us (99%)
    pallas_call x1, Pallas kernels, per_device(): pl.pallas_call(gather_kernel, name='gather', out_shape=[jax.ShapeDtypeStr...  547 us
    pallas_call x1, Pallas kernels, per_device(): pl.pallas_call(update_kernel, name='update', out_shape=jax.ShapeDtypeStru...  73.6 us

profile of v1, /device:TPU:26, one launch (start us, length us, event | category | flops | bytes accessed | tf_op | source)
XLA Modules:
  0.0 626.1 jit_solution(15833975220123271825)
XLA Ops:
  0.0 546.6 %gather.1 = (f32[8,1024,128]{2,1,0:T(8,128)S(1)}, f32[8,128,1024]{2,1,0:T(8,128)S(1)}, f32[8,8,128,128]{3,2,1,0:T(8,128)S(1)}) custom-call(f32[1024,1024]{1,0:T(8,128)} %t_ref.3), custom_call_target="tpu_custom_call" | custom-call | tf_op jit(solution)/shard_map/gather/pallas_call | solution.py:397
  546.6 0.0 copy-start
  546.6 1.9 copy-done
  548.6 0.0 copy-start.1
  548.6 2.0 copy-done.1
  550.5 0.0 copy-start.2
  550.5 1.9 copy-done.2
  552.5 73.6 %update.1 = f32[1024,1024]{1,0:T(8,128)} custom-call(f32[1024,1024]{1,0:T(8,128)} %t_ref.3, f32[8,1024,128]{2,1,0:T(8,128)} %copy-done, f32[8,128,1024]{2,1,0:T(8,128)} %copy-done.1, f32[8,8,128,128]{3,2,1,0:T(8,128)} %copy-done.2), custom_call_target="tpu_custom_call" | custom-call | tf_op jit(solution)/shard_map/update/pallas_call | solution.py:414
Async XLA Ops:
  546.6 1.9 copy-start
  548.6 2.0 copy-start.1
  550.5 1.9 copy-start.2

commit v2 on v0

v2 whole, which is shorter than its diff:
```python
import functools

import jax
import jax.numpy as jnp
from jax import lax
from jax.experimental import pallas as pl
from jax.experimental.pallas import tpu as pltpu
from jax.sharding import PartitionSpec as P

BLOCK = 128
STEPS = 8
WIDTH = BLOCK * STEPS
TILE = 8
TILES = BLOCK // TILE
SIDE = 4
RING = 8
CHUNKS = 8
WIDE = 2 * BLOCK
ROUNDS = WIDTH // WIDE

UP_FIRST = ((0, 1, 2, 3, 4), (1, 2, 3, 4), (2, 3, 4, 5, 6), (3, 4, 5, 6, 7))
DOWN_FIRST = ((0, 7, 6, 5), (1, 0, 7, 6, 5), (2, 1, 0, 7), (3, 2, 1, 0))
UP = ((0, 1, 2), (1, 2, 3), (2, 3, 4, 5, 6, 7), (3, 4, 5, 6, 7, 0))
DOWN = ((0, 7, 6, 5, 4, 3), (1, 0, 7, 6, 5, 4), (2, 1, 0), (3, 2, 1))


def any_of(value, choices):
    hit = value == choices[0]
    for choice in choices[1:]:
        hit = hit | (value == choice)
    return hit


def table(value, entries):
    out = jnp.int32(entries[0])
    for n, entry in enumerate(entries[1:], 1):
        out = jnp.where(value == n, jnp.int32(entry), out)
    return out


def hops(ups, downs, m):
    return [ups[m].index(z) if z in ups[m] else downs[m].index(z) for z in range(RING)]


class Links:
    def __init__(self, ap, aq, wb, zsem, zsend, qsem, qsend, wsem, wsend):
        self.ap, self.aq, self.wb = ap, aq, wb
        self.zsem, self.zsend = zsem, zsend
        self.qsem, self.qsend = qsem, qsend
        self.wsem, self.wsend = wsem, wsend
        self.p, self.q = lax.axis_index("prow"), lax.axis_index("pcol")
        self.y, self.x = self.p // SIDE, self.p % SIDE
        self.z, self.c = self.q // 2, self.q % 2
        self.zhops = [table(self.z, hops(UP, DOWN, m)) for m in range(4)]
        self.zfirst = [table(self.z, hops(UP_FIRST, DOWN_FIRST, m)) for m in range(4)]
        self.up = [any_of(self.z, UP[m][:-1]) for m in range(4)]
        self.down = [any_of(self.z, DOWN[m][:-1]) for m in range(4)]
        self.up_first = [any_of(self.z, UP_FIRST[m][:-1]) for m in range(4)]
        self.down_first = [any_of(self.z, DOWN_FIRST[m][:-1]) for m in range(4)]
        self.qhops, self.qways = [], []
        for i in range(STEPS):
            ys, dx = i // SIDE, (self.x - i % SIDE + SIDE) % SIDE
            own, same = self.y == ys, dx == 0
            self.qhops.append(table(self.y, (0, 1, 2, 1) if ys == 0 else (1, 0, 1, 2)) + table(dx, (0, 1, 2, 1)))
            if ys == 0:
                ways = (same & own, same & (own | (self.y == 3)), same | (dx == 1), same)
            else:
                ways = (same & (own | (self.y == 2)), same & own, same, same | (dx == 3))
            self.qways.append(ways)

    def device(self, dx=0, dy=0, dz=0, dc=0):
        prow = (self.y + dy) % SIDE * SIDE + (self.x + dx) % SIDE
        pcol = (self.z + dz) % RING * 2 + (self.c + dc) % 2
        return (prow, pcol)

    def neighbours(self):
        around = [self.device(dx=n) for n in (1, 2, 3)] + [self.device(dy=n) for n in (1, 2, 3)]
        return around + [self.device(dz=1), self.device(dz=RING - 1), self.device(dc=1)]

    def copy(self, src, dst, send, recv, device):
        return pltpu.make_async_remote_copy(
            src_ref=src, dst_ref=dst, send_sem=send, recv_sem=recv,
            device_id=device, device_id_type=pl.DeviceIdType.MESH,
        )

    def zcopy(self, way, m, t, parity, first=False):
        j = 2 * m + parity
        device = (self.device(dz=1), self.device(dz=RING - 1), self.device(dc=1))[way]
        part = self.ap.at[j, pl.ds(0 if first else pl.multiple_of(t * BLOCK, BLOCK), BLOCK)]
        return self.copy(part, part, self.zsend.at[int(first), way, m], self.zsem.at[j, t], device)

    def zitem(self, m, t, first=False):
        up, down = (self.up_first, self.down_first) if first else (self.up, self.down)

        @pl.when(self.z != m)
        def _():
            self.zcopy(0, m, t, self.c, first).wait_recv()

        for way, sends in enumerate((up[m], down[m])):
            @pl.when(sends)
            def _():
                self.zcopy(way, m, t, self.c, first).start()

        self.zcopy(2, m, t, self.c, first).start()

    def zslot(self, slot):
        for m in range(4):
            t = slot - self.zhops[m]

            @pl.when((t >= 1) & (t < CHUNKS))
            def _():
                self.zitem(m, t)

    def ztwin(self, m, t, first=False):
        self.zcopy(2, m, t, 1 - self.c, first).wait_recv()

    def qcopy(self, way, i, t):
        device = (self.device(dy=1), self.device(dy=3), self.device(dx=1), self.device(dx=3))[way]
        part = self.aq.at[i, t]
        return self.copy(part, part, self.qsend.at[way, i], self.qsem.at[i, t], device)

    def qslot(self, slot):
        for i in range(STEPS):
            t = slot - self.qhops[i]

            @pl.when((t >= 0) & (t < CHUNKS))
            def _():
                @pl.when(self.p != i)
                def _():
                    self.qcopy(0, i, t).wait_recv()

                for way, sends in enumerate(self.qways[i]):
                    @pl.when(sends)
                    def _():
                        self.qcopy(way, i, t).start()

    def wcopy(self, way, k, m, parity, own=False):
        step = way % 3 + 1
        device = self.device(dc=1) if way == 6 else self.device(dy=step) if way >= 3 else self.device(dx=step)
        j = 2 * m + parity
        dst = self.wb.at[k, j]
        src = self.ap.at[j, pl.ds(0, BLOCK)] if own else dst
        return self.copy(src, dst, self.wsend.at[way, k], self.wsem.at[k, j], device)

    def wsource(self, k):
        @pl.when(self.p == k)
        def _():
            for m in range(k // 2, STEPS // 2):
                for way in range(6):
                    self.wcopy(way, k, m, self.c, own=True).start()

    def wrow(self, k):
        @pl.when((self.y == k // SIDE) & (self.p != k))
        def _():
            for m in range(k // 2, STEPS // 2):
                self.wcopy(0, k, m, self.c).wait_recv()
                for way in (3, 4, 5, 6):
                    self.wcopy(way, k, m, self.c).start()

    def wrest(self, k):
        @pl.when(self.y != k // SIDE)
        def _():
            def item(m, carry):
                self.wcopy(0, k, m, self.c).wait_recv()
                self.wcopy(6, k, m, self.c).start()
                return carry

            lax.fori_loop(k // 2, STEPS // 2, item, 0)

    def wtwin(self, k):
        @pl.when(self.p != k)
        def _():
            def item(m, carry):
                self.wcopy(6, k, m, 1 - self.c).wait_recv()
                return carry

            lax.fori_loop(k // 2, STEPS // 2, item, 0)

    def drain(self):
        for m in range(4):
            for way, first, later in (
                (0, self.up_first[m], self.up[m]), (1, self.down_first[m], self.down[m]), (2, None, None),
            ):
                device = self.device(dc=1)
                one, rest = self.ap.at[0, pl.ds(0, BLOCK)], self.ap.at[0, pl.ds(0, WIDTH - BLOCK)]
                head = self.copy(one, one, self.zsend.at[1, way, m], self.zsem.at[0, 0], device)
                tail = self.copy(rest, rest, self.zsend.at[0, way, m], self.zsem.at[0, 0], device)
                if first is None:
                    head.wait_send()
                    tail.wait_send()
                else:
                    pl.when(first)(head.wait_send)
                    pl.when(later)(tail.wait_send)
        for i in range(STEPS):
            for way, sends in enumerate(self.qways[i]):
                whole = self.copy(
                    self.aq.at[i], self.aq.at[i], self.qsend.at[way, i], self.qsem.at[0, 0], self.device(dc=1)
                )
                pl.when(sends)(whole.wait_send)
        for k in range(STEPS):
            part = self.wb.at[k, pl.ds(0, STEPS // 2 - k // 2)]
            for way in range(7):
                sends = (self.p == k) if way < 3 else (self.y == k // SIDE) if way < 6 else (self.p != k)
                whole = self.copy(part, part, self.wsend.at[way, k], self.wsem.at[0, 0], self.device(dc=1))
                pl.when(sends)(whole.wait_send)


def row_of(x, j):
    return jnp.broadcast_to(x[j : j + 1, :], (TILE, BLOCK))


def lane_of(x, c):
    return jnp.broadcast_to(x[:, c : c + 1], x.shape)


def times(x, n):
    return x if n == 1 else jnp.concatenate([x] * n, axis=0)


def invert_factor(block):
    sub = lax.broadcasted_iota(jnp.int32, (TILE, BLOCK), 0)
    rows = lax.broadcasted_iota(jnp.int32, (BLOCK, BLOCK), 0)
    lanes = lax.broadcasted_iota(jnp.int32, (BLOCK, BLOCK), 1)
    ident = jnp.where(rows == lanes, 1.0, 0.0).astype(jnp.float32)
    head, rest = block[:TILE], block[TILE:]
    bhead, brest = ident[:TILE], ident[TILE:]
    done = []
    ahead = [lane_of(head, j) for j in range(TILE)]
    for s in range(TILES):
        left = TILES - 1 - s
        first = TILE * s
        col = ahead
        if left:
            below = [lane_of(rest, first + j) for j in range(TILE)]
            ahead = [lane_of(rest[:TILE], first + TILE + j) for j in range(TILE)]
        r, b = head, bhead
        scale, coef = [], {}
        for j in range(TILE):
            scale.append(lax.rsqrt(row_of(col[j], j)))
            line = col[j] * scale[j]
            for k in range(j + 1, TILE):
                coef[j, k] = row_of(line, k)
                col[k] = col[k] - line * coef[j, k]
            ru, bu = row_of(r, j) * scale[j], row_of(b, j) * scale[j]
            if j < TILE - 1:
                low = jnp.where(sub > j, line, 0.0)
                r = jnp.where(sub == j, ru, r - low * ru)
                b = jnp.where(sub == j, bu, b - low * bu)
            else:
                r = jnp.where(sub == j, ru, r)
                b = jnp.where(sub == j, bu, b)
        done.append(b)
        if not left:
            break
        lines = []
        for j in range(TILE):
            line = below[j] * times(scale[j], left)
            lines.append(line)
            for k in range(j + 1, TILE):
                below[k] = below[k] - line * times(coef[j, k], left)
        for m in range(TILE):
            near = lines[m][:TILE]
            for j in range(TILE):
                ahead[j] = ahead[j] - near * row_of(near, j)
        for j in range(TILE):
            rest = rest - lines[j] * times(row_of(r, j), left)
            brest = brest - lines[j] * times(row_of(b, j), left)
        head, rest = rest[:TILE], rest[TILE:]
        bhead, brest = brest[:TILE], brest[TILE:]
    return jnp.concatenate(done, axis=0)


def split(x):
    high = x.astype(jnp.bfloat16)
    return high, (x - high.astype(jnp.float32)).astype(jnp.bfloat16)


NN = (((1,), (0,)), ((), ()))
TN = (((0,), (0,)), ((), ()))
NT = (((1,), (1,)), ((), ()))


def dot3(a, b, dims):
    one = functools.partial(lax.dot_general, dimension_numbers=dims, preferred_element_type=jnp.float32)
    return one(a[0], b[0]) + one(a[0], b[1]) + one(a[1], b[0])


def kernel(t_ref, out, ap, aq, wb, tv, lpf, uh, ul, xh, xl, lph, lpl, lqh, lql, diag, lsem, osem, *sems):
    net = Links(ap, aq, wb, *sems)
    p, q = net.p, net.q
    barrier = pltpu.get_barrier_semaphore()
    for device in net.neighbours():
        pl.semaphore_signal(barrier, inc=1, device_id=device, device_id_type=pl.DeviceIdType.MESH)
    cols = pl.ds(0, BLOCK)
    head = pltpu.make_async_copy(t_ref.at[cols, cols], ap.at[q % STEPS, cols], lsem.at[0])
    later = pl.ds(BLOCK, WIDTH - BLOCK)
    body = pltpu.make_async_copy(t_ref.at[later, cols], ap.at[q % STEPS, later], lsem.at[1])
    rows = [
        pltpu.make_async_copy(t_ref.at[cols, pl.ds(t * BLOCK, BLOCK)], aq.at[p % STEPS, t], lsem.at[2 + t])
        for t in range(CHUNKS)
    ]
    whole = pltpu.make_async_copy(t_ref, tv, lsem.at[2 + CHUNKS])

    @pl.when(q < STEPS)
    def _():
        head.start()
        body.start()

    @pl.when(p < STEPS)
    def _():
        for row in rows:
            row.start()

    whole.start()
    pl.semaphore_wait(barrier, 9)

    @pl.when(q < STEPS)
    def _():
        head.wait()
        body.wait()

    @pl.when(p < STEPS)
    def _():
        for row in rows:
            row.wait()

    for slot in range(5):
        for m in range(4):
            @pl.when(net.zfirst[m] == slot)
            def _():
                net.zitem(m, 0, first=True)
    for k in range(STEPS):
        net.wsource(k)
    for m in range(4):
        net.ztwin(m, 0, first=True)
    for k in range(STEPS):
        @pl.when(p == k)
        def _():
            for j in range(STEPS):
                wb[k, j] = ap[j, 0:BLOCK]
    for k in range(STEPS):
        net.wrow(k)
    xh[...] = jnp.zeros_like(xh)
    xl[...] = jnp.zeros_like(xl)
    net.wrest(0)
    net.wtwin(0)
    diag[...] = wb[0, 0]

    def step(k, carry):
        net.zslot(k + 1)
        net.qslot(k)

        @pl.when(k < STEPS - 1)
        def _():
            net.wrest(k + 1)

        inv = invert_factor(diag[...])

        @pl.when(k < STEPS - 1)
        def _():
            net.wtwin(k + 1)

        ih, il = split(inv)
        for kk in range(STEPS):
            lo, hi = kk * BLOCK, (kk + 1) * BLOCK

            @pl.when(k == kk)
            def _():
                xh[lo:hi, lo:hi] = ih
                xl[lo:hi, lo:hi] = il
                if kk:
                    lead = (uh[:lo, lo:hi], ul[:lo, lo:hi])
                    gx = split(dot3(lead, (xh[:lo, :lo], xl[:lo, :lo]), TN))
                    xrow = split(-dot3((ih, il), gx, NN))
                    xh[lo:hi, :lo], xl[lo:hi, :lo] = xrow
                if kk < STEPS - 1:
                    g = jnp.concatenate([wb[kk, j] for j in range(kk + 1, STEPS)], axis=1)
                    if kk:
                        g = g - dot3(lead, (uh[:lo, hi:], ul[:lo, hi:]), TN)
                    urow = split(dot3((ih, il), split(g), NN))
                    uh[lo:hi, hi:], ul[lo:hi, hi:] = urow
                    nxt = (uh[:hi, hi : hi + BLOCK], ul[:hi, hi : hi + BLOCK])
                    diag[...] = wb[kk + 1, kk + 1] - dot3(nxt, nxt, TN)

        return carry

    lax.fori_loop(0, STEPS, step, 0)
    whole.wait()

    def spread(u, carry):
        net.zslot(9 + 2 * u)
        net.qslot(8 + 2 * u)
        net.zslot(10 + 2 * u)
        net.qslot(9 + 2 * u)
        for m in range(4):
            pl.when(u > 0)(lambda: net.ztwin(m, 2 * u))
            net.ztwin(m, 2 * u + 1)
        mine = pl.ds(pl.multiple_of(u * WIDE, WIDE), WIDE)
        apu = split(jnp.concatenate([ap[j, mine] for j in range(STEPS)], axis=1))
        aqu = split(jnp.concatenate(
            [jnp.concatenate([aq[i, 2 * u], aq[i, 2 * u + 1]], axis=1) for i in range(STEPS)], axis=0))
        for b in range(ROUNDS):
            lo, hi = b * WIDE, (b + 1) * WIDE
            xb = (xh[lo:hi, :hi], xl[lo:hi, :hi])
            lp = dot3((apu[0][:, :hi], apu[1][:, :hi]), xb, NT)
            lpf[2 * b, mine] = lp[:, :BLOCK]
            lpf[2 * b + 1, mine] = lp[:, BLOCK:]
            lph[u, :, lo:hi], lpl[u, :, lo:hi] = split(lp)
            lqh[u, lo:hi, :], lql[u, lo:hi, :] = split(dot3(xb, (aqu[0][:hi], aqu[1][:hi]), NN))

        def cell(a, b):
            where = (pl.ds(pl.multiple_of(a * WIDE, WIDE), WIDE), pl.ds(pl.multiple_of(b * WIDE, WIDE), WIDE))
            tv[where] = tv[where] - dot3((lph[a], lpl[a]), (lqh[b], lql[b]), NN)

        def cells(v, carry):
            cell(u, v)
            cell(v, u)
            return carry

        lax.fori_loop(0, u, cells, 0)
        cell(u, u)
        return carry

    lax.fori_loop(0, ROUNDS, spread, 0)

    @pl.when(p < STEPS)
    def _():
        tv[0:BLOCK, :] = jnp.zeros((BLOCK, WIDTH), jnp.float32)

    @pl.when(q < STEPS)
    def _():
        tv[BLOCK:, 0:BLOCK] = lpf[q % STEPS, BLOCK:]
        top = lpf[q % STEPS, 0:BLOCK]
        down = lax.broadcasted_iota(jnp.int32, (BLOCK, BLOCK), 0) + p * BLOCK
        across = lax.broadcasted_iota(jnp.int32, (BLOCK, BLOCK), 1) + q * BLOCK
        tv[0:BLOCK, 0:BLOCK] = jnp.where((p >= STEPS) | (down >= across), top, 0.0)

    result = pltpu.make_async_copy(tv, out, osem)
    result.start()
    net.drain()
    result.wait()


def per_device(blocked):
    f32, bf16 = jnp.float32, jnp.bfloat16
    hbm = pl.BlockSpec(memory_space=pl.ANY)
    dma, square = pltpu.SemaphoreType.DMA, (WIDTH, WIDTH)
    return pl.pallas_call(
        kernel,
        name="factor",
        out_shape=jax.ShapeDtypeStruct(square, f32),
        in_specs=[hbm],
        out_specs=hbm,
        scratch_shapes=[
            pltpu.VMEM((STEPS, WIDTH, BLOCK), f32),
            pltpu.VMEM((STEPS, CHUNKS, BLOCK, BLOCK), f32),
            pltpu.VMEM((STEPS, STEPS, BLOCK, BLOCK), f32),
            pltpu.VMEM(square, f32),
            pltpu.VMEM((STEPS, WIDTH, BLOCK), f32),
            *(pltpu.VMEM(square, bf16) for _ in range(4)),
            *(pltpu.VMEM((ROUNDS, WIDE, WIDTH), bf16) for _ in range(2)),
            *(pltpu.VMEM((ROUNDS, WIDTH, WIDE), bf16) for _ in range(2)),
            pltpu.VMEM((BLOCK, BLOCK), f32),
            dma((3 + CHUNKS,)), dma,
            dma((STEPS, CHUNKS)), dma((2, 3, 4)),
            dma((STEPS, CHUNKS)), dma((4, STEPS)),
            dma((STEPS, STEPS)), dma((7, STEPS)),
        ],
        compiler_params=pltpu.CompilerParams(collective_id=0, has_side_effects=True, vmem_limit_bytes=58 << 20),
    )(blocked)


def solution(mesh):
    return jax.shard_map(
        per_device,
        mesh=mesh,
        in_specs=(P("prow", "pcol"),),
        out_specs=P("prow", "pcol"),
        check_vma=False,
    )
```

time: 700 us -> 135 us (0.19)
  the two profiles are of different devices: /device:TPU:2 before, /device:TPU:16 now
where the time goes in v2:
time: 135 us
  Pallas kernels  130 us (96%)
  local copies, waits for them, and re-layouts  4.79 us (4%)
    pallas_call x1, Pallas kernels, per_device(): pl.pallas_call(kernel, name='factor', out_shape=jax.ShapeDtypeStruct(squa...  130 us
    unnamed x1, local copies, waits for them, and re-layouts  4.79 us

profile of v2, /device:TPU:16, one launch (start us, length us, event | category | flops | bytes accessed | tf_op | source)
XLA Modules:
  0.0 134.7 jit_solution(13636339837021592367)
XLA Ops:
  0.0 129.9 %factor.1 = f32[1024,1024]{1,0:T(8,128)} custom-call(f32[1024,1024]{1,0:T(8,128)} %t_ref.1), custom_call_target="tpu_custom_call" | custom-call | tf_op jit(solution)/shard_map/factor/pallas_call | solution.py:448
  129.9 4.8 %copy.3 = f32[1024,1024]{1,0:T(8,128)} copy(f32[1024,1024]{1,0:T(8,128)} %factor.1) | data formatting | bytes 8388608

commit v3 on v2

--- a/solution.py
+++ b/solution.py
@@ -15,6 +15,12 @@
 SIDE = 4
 RING = 8
 CHUNKS = 8
+STAGGER = 1
+BEFORE = 5
+EXTRA = 2
+START = 3
+AFTER = 0
+PASS = (1, 2, 4)
 WIDE = 2 * BLOCK
 ROUNDS = WIDTH // WIDE
 
@@ -43,11 +49,11 @@
 
 
 class Links:
-    def __init__(self, ap, aq, wb, zsem, zsend, qsem, qsend, wsem, wsend):
+    def __init__(self, ap, aq, wb, zsem, zsend, qsem, qsend, wsem, wsend, fsend):
         self.ap, self.aq, self.wb = ap, aq, wb
         self.zsem, self.zsend = zsem, zsend
         self.qsem, self.qsend = qsem, qsend
-        self.wsem, self.wsend = wsem, wsend
+        self.wsem, self.wsend, self.fsend = wsem, wsend, fsend
         self.p, self.q = lax.axis_index("prow"), lax.axis_index("pcol")
         self.y, self.x = self.p // SIDE, self.p % SIDE
         self.z, self.c = self.q // 2, self.q % 2
@@ -57,16 +63,20 @@
         self.down = [any_of(self.z, DOWN[m][:-1]) for m in range(4)]
         self.up_first = [any_of(self.z, UP_FIRST[m][:-1]) for m in range(4)]
         self.down_first = [any_of(self.z, DOWN_FIRST[m][:-1]) for m in range(4)]
-        self.qhops, self.qways = [], []
+        self.beside = (self.device(dy=1), self.device(dy=3), self.device(dx=1), self.device(dx=3))
+        self.along = (self.device(dz=1), self.device(dz=RING - 1), self.device(dc=1))
+        self.qhops, self.ways = [], []
         for i in range(STEPS):
             ys, dx = i // SIDE, (self.x - i % SIDE + SIDE) % SIDE
-            own, same = self.y == ys, dx == 0
+            row, same = self.y == ys, dx == 0
             self.qhops.append(table(self.y, (0, 1, 2, 1) if ys == 0 else (1, 0, 1, 2)) + table(dx, (0, 1, 2, 1)))
-            if ys == 0:
-                ways = (same & own, same & (own | (self.y == 3)), same | (dx == 1), same)
-            else:
-                ways = (same & (own | (self.y == 2)), same & own, same, same | (dx == 3))
-            self.qways.append(ways)
+            turn = row | (self.y == (3 if ys == 0 else 2))
+            on = same | (dx == (1 if ys == 0 else 3))
+            ways = []
+            for down, across in ((same, True), (True, row)):
+                one, two = (row & down, turn & down), (on & across, same & across)
+                ways.append((*(one if ys == 0 else one[::-1]), *(two if ys == 0 else two[::-1])))
+            self.ways.append(ways)
 
     def device(self, dx=0, dy=0, dz=0, dc=0):
         prow = (self.y + dy) % SIDE * SIDE + (self.x + dx) % SIDE
@@ -75,7 +85,7 @@
 
     def neighbours(self):
         around = [self.device(dx=n) for n in (1, 2, 3)] + [self.device(dy=n) for n in (1, 2, 3)]
-        return around + [self.device(dz=1), self.device(dz=RING - 1), self.device(dc=1)]
+        return around + [self.device(dz=n) for n in range(1, RING)] + [self.device(dc=1)]
 
     def copy(self, src, dst, send, recv, device):
         return pltpu.make_async_remote_copy(
@@ -85,9 +95,8 @@
 
     def zcopy(self, way, m, t, parity, first=False):
         j = 2 * m + parity
-        device = (self.device(dz=1), self.device(dz=RING - 1), self.device(dc=1))[way]
         part = self.ap.at[j, pl.ds(0 if first else pl.multiple_of(t * BLOCK, BLOCK), BLOCK)]
-        return self.copy(part, part, self.zsend.at[int(first), way, m], self.zsem.at[j, t], device)
+        return self.copy(part, part, self.zsend.at[int(first), way, m], self.zsem.at[j, t], self.along[way])
 
     def zitem(self, m, t, first=False):
         up, down = (self.up_first, self.down_first) if first else (self.up, self.down)
@@ -114,10 +123,9 @@
     def ztwin(self, m, t, first=False):
         self.zcopy(2, m, t, 1 - self.c, first).wait_recv()
 
-    def qcopy(self, way, i, t):
-        device = (self.device(dy=1), self.device(dy=3), self.device(dx=1), self.device(dx=3))[way]
+    def qcopy(self, way, i, t, order=0):
         part = self.aq.at[i, t]
-        return self.copy(part, part, self.qsend.at[way, i], self.qsem.at[i, t], device)
+        return self.copy(part, part, self.qsend.at[order, way, i], self.qsem.at[i, t], self.beside[way])
 
     def qslot(self, slot):
         for i in range(STEPS):
@@ -129,52 +137,85 @@
                 def _():
                     self.qcopy(0, i, t).wait_recv()
 
-                for way, sends in enumerate(self.qways[i]):
-                    @pl.when(sends)
+                odd = t % 2
+                for way, (even_sends, odd_sends) in enumerate(zip(*self.ways[i])):
+                    @pl.when(jnp.where(odd == 1, odd_sends, even_sends))
                     def _():
-                        self.qcopy(way, i, t).start()
+                        self.qcopy(way, i, t, odd).start()
 
     def wcopy(self, way, k, m, parity, own=False):
-        step = way % 3 + 1
-        device = self.device(dc=1) if way == 6 else self.device(dy=step) if way >= 3 else self.device(dx=step)
+        device = self.along[2] if way == 4 else self.beside[way]
         j = 2 * m + parity
         dst = self.wb.at[k, j]
         src = self.ap.at[j, pl.ds(0, BLOCK)] if own else dst
-        return self.copy(src, dst, self.wsend.at[way, k], self.wsem.at[k, j], device)
-
-    def wsource(self, k):
-        @pl.when(self.p == k)
+        send = self.wsend.at[way, m * (m + 1) - 2 + k]
+        return self.copy(src, dst, send, self.wsem.at[k, j], device)
+
+    def wneeded(self, k, m):
+        return self.c == 1 if k == 2 * m + 1 else self.c >= 0
+
+    def wslot(self, slot):
+        for m in range(1, 4):
+            for k in range(2 * m + 2):
+                @pl.when((self.zfirst[m] + self.qhops[k] + STAGGER * (m - 1) == slot) & self.wneeded(k, m))
+                def _():
+                    @pl.when(self.p == k)
+                    def _():
+                        for way in range(4):
+                            pl.when(self.ways[k][0][way])(self.wcopy(way, k, m, self.c, own=True).start)
+
+                    @pl.when(self.p != k)
+                    def _():
+                        self.wcopy(0, k, m, self.c).wait_recv()
+                        for way in range(4):
+                            pl.when(self.ways[k][0][way])(self.wcopy(way, k, m, self.c).start)
+                        self.wcopy(4, k, m, self.c).start()
+
+    def fcopy(self, n, k, parity, own=False):
+        if n < 7:
+            device = self.device(dz=(4, 3, 5, 2, 6, 1, 7)[n])
+        elif n < 13:
+            step = (2, 1, 3)[(n - 7) % 3]
+            device = self.device(dy=step) if n < 10 else self.device(dx=step)
+        else:
+            device = self.along[2]
+        dst = self.wb.at[k, parity]
+        src = self.ap.at[parity, pl.ds(0, BLOCK)] if own else dst
+        return self.copy(src, dst, self.fsend.at[n, k], self.wsem.at[k, parity], device)
+
+    def fsource(self):
+        for k in range(2):
+            @pl.when((self.p == k) & (self.z == 0) & (k <= self.c))
+            def _():
+                for n in range(14):
+                    self.fcopy(n, k, self.c, own=True).start()
+
+    def fpass(self, stage):
+        for k in range(2):
+            needed = k <= self.c
+            if stage == 0:
+                here, sends = (self.p == k) & (self.z != 0), range(7, 14)
+            elif stage == 1:
+                here, sends = (self.x == k) & (self.y != 0), range(10, 14)
+            else:
+                here, sends = self.x != k, range(13, 14)
+
+            @pl.when(here & needed)
+            def _():
+                self.fcopy(0, k, self.c).wait_recv()
+                for n in sends:
+                    self.fcopy(n, k, self.c).start()
+
+    def wtwin(self, j):
+        @pl.when(self.c != j % 2)
         def _():
-            for m in range(k // 2, STEPS // 2):
-                for way in range(6):
-                    self.wcopy(way, k, m, self.c, own=True).start()
-
-    def wrow(self, k):
-        @pl.when((self.y == k // SIDE) & (self.p != k))
-        def _():
-            for m in range(k // 2, STEPS // 2):
-                self.wcopy(0, k, m, self.c).wait_recv()
-                for way in (3, 4, 5, 6):
-                    self.wcopy(way, k, m, self.c).start()
-
-    def wrest(self, k):
-        @pl.when(self.y != k // SIDE)
-        def _():
-            def item(m, carry):
-                self.wcopy(0, k, m, self.c).wait_recv()
-                self.wcopy(6, k, m, self.c).start()
+            def item(k, carry):
+                part = self.wb.at[k, j]
+                twin = self.copy(part, part, self.fsend.at[0, 0], self.wsem.at[k, j], self.along[2])
+                pl.when((j < 2) | (self.p != k))(twin.wait_recv)
                 return carry
 
-            lax.fori_loop(k // 2, STEPS // 2, item, 0)
-
-    def wtwin(self, k):
-        @pl.when(self.p != k)
-        def _():
-            def item(m, carry):
-                self.wcopy(6, k, m, 1 - self.c).wait_recv()
-                return carry
-
-            lax.fori_loop(k // 2, STEPS // 2, item, 0)
+            lax.fori_loop(0, j + 1, item, 0)
 
     def drain(self):
         for m in range(4):
@@ -192,17 +233,20 @@
                     pl.when(first)(head.wait_send)
                     pl.when(later)(tail.wait_send)
         for i in range(STEPS):
-            for way, sends in enumerate(self.qways[i]):
-                whole = self.copy(
-                    self.aq.at[i], self.aq.at[i], self.qsend.at[way, i], self.qsem.at[0, 0], self.device(dc=1)
-                )
-                pl.when(sends)(whole.wait_send)
-        for k in range(STEPS):
-            part = self.wb.at[k, pl.ds(0, STEPS // 2 - k // 2)]
-            for way in range(7):
-                sends = (self.p == k) if way < 3 else (self.y == k // SIDE) if way < 6 else (self.p != k)
-                whole = self.copy(part, part, self.wsend.at[way, k], self.wsem.at[0, 0], self.device(dc=1))
-                pl.when(sends)(whole.wait_send)
+            half = self.aq.at[i, pl.ds(0, CHUNKS // 2)]
+            for order in range(2):
+                for way, sends in enumerate(self.ways[i][order]):
+                    every = self.copy(half, half, self.qsend.at[order, way, i], self.qsem.at[0, 0], self.beside[way])
+                    pl.when(sends)(every.wait_send)
+        for m in range(1, 4):
+            for k in range(2 * m + 2):
+                for way in range(5):
+                    sends = self.ways[k][0][way] if way < 4 else self.p != k
+                    pl.when(sends & self.wneeded(k, m))(self.wcopy(way, k, m, self.c).wait_send)
+        for k in range(2):
+            for n in range(14):
+                line = (self.p == k) & (self.z == 0) if n < 7 else self.p == k if n < 10 else self.x == k if n < 13 else True
+                pl.when(line & (k <= self.c))(self.fcopy(n, k, self.c).wait_send)
 
 
 def row_of(x, j):
@@ -285,7 +329,7 @@
     return one(a[0], b[0]) + one(a[0], b[1]) + one(a[1], b[0])
 
 
-def kernel(t_ref, out, ap, aq, wb, tv, lpf, uh, ul, xh, xl, lph, lpl, lqh, lql, diag, lsem, osem, *sems):
+def kernel(t_ref, out, ap, aq, wb, tv, lpf, xh, xl, gx, lph, lpl, lqh, lql, diag, lsem, osem, *sems):
     net = Links(ap, aq, wb, *sems)
     p, q = net.p, net.q
     barrier = pltpu.get_barrier_semaphore()
@@ -312,7 +356,7 @@
             row.start()
 
     whole.start()
-    pl.semaphore_wait(barrier, 9)
+    pl.semaphore_wait(barrier, 14)
 
     @pl.when(q < STEPS)
     def _():
@@ -324,43 +368,58 @@
         for row in rows:
             row.wait()
 
-    for slot in range(5):
+    xh[...] = jnp.zeros_like(xh)
+    xl[...] = jnp.zeros_like(xl)
+
+    net.fsource()
+
+    def first(slot, carry):
         for m in range(4):
-            @pl.when(net.zfirst[m] == slot)
-            def _():
-                net.zitem(m, 0, first=True)
-    for k in range(STEPS):
-        net.wsource(k)
+            pl.when(net.zfirst[m] == slot)(functools.partial(net.zitem, m, 0, True))
+        net.wslot(slot)
+        net.zslot(slot - START + 1)
+        net.qslot(slot - START)
+        for stage, at in enumerate(PASS):
+            pl.when(slot == at)(functools.partial(net.fpass, stage))
+        return carry
+
+    lax.fori_loop(0, BEFORE, first, 0)
     for m in range(4):
         net.ztwin(m, 0, first=True)
     for k in range(STEPS):
         @pl.when(p == k)
         def _():
-            for j in range(STEPS):
+            for j in range(max(k, 2), STEPS):
                 wb[k, j] = ap[j, 0:BLOCK]
-    for k in range(STEPS):
-        net.wrow(k)
-    xh[...] = jnp.zeros_like(xh)
-    xl[...] = jnp.zeros_like(xl)
-    net.wrest(0)
-    net.wtwin(0)
-    diag[...] = wb[0, 0]
+
+    for k in range(2):
+        @pl.when((p == k) & (net.z == 0) & (k <= net.c))
+        def _():
+            wb[k, net.c] = ap[net.c, 0:BLOCK]
 
     def step(k, carry):
-        net.zslot(k + 1)
-        net.qslot(k)
-
-        @pl.when(k < STEPS - 1)
-        def _():
-            net.wrest(k + 1)
-
-        inv = invert_factor(diag[...])
-
-        @pl.when(k < STEPS - 1)
-        def _():
-            net.wtwin(k + 1)
-
-        ih, il = split(inv)
+        def catch_up(slot, carry):
+            net.wslot(slot)
+            net.zslot(slot - START + 1)
+            net.qslot(slot - START)
+            return carry
+
+        lax.fori_loop(BEFORE + k + jnp.minimum(k, EXTRA), BEFORE + k + 1 + jnp.minimum(k + 1, EXTRA), catch_up, 0)
+        net.wtwin(k)
+        for kk in range(STEPS):
+            lo, hi = kk * BLOCK, (kk + 1) * BLOCK
+
+            @pl.when(k == kk)
+            def _():
+                if kk:
+                    x = (xh[:lo, :lo], xl[:lo, :lo])
+                    col = split(dot3(x, split(wb[0:kk, kk].reshape(lo, BLOCK)), NN))
+                    diag[...] = wb[kk, kk] - dot3(col, col, TN)
+                    gx[:, :lo] = dot3(col, x, TN)
+                else:
+                    diag[...] = wb[0, 0]
+
+        ih, il = split(invert_factor(diag[...]))
         for kk in range(STEPS):
             lo, hi = kk * BLOCK, (kk + 1) * BLOCK
 
@@ -369,18 +428,7 @@
                 xh[lo:hi, lo:hi] = ih
                 xl[lo:hi, lo:hi] = il
                 if kk:
-                    lead = (uh[:lo, lo:hi], ul[:lo, lo:hi])
-                    gx = split(dot3(lead, (xh[:lo, :lo], xl[:lo, :lo]), TN))
-                    xrow = split(-dot3((ih, il), gx, NN))
-                    xh[lo:hi, :lo], xl[lo:hi, :lo] = xrow
-                if kk < STEPS - 1:
-                    g = jnp.concatenate([wb[kk, j] for j in range(kk + 1, STEPS)], axis=1)
-                    if kk:
-                        g = g - dot3(lead, (uh[:lo, hi:], ul[:lo, hi:]), TN)
-                    urow = split(dot3((ih, il), split(g), NN))
-                    uh[lo:hi, hi:], ul[lo:hi, hi:] = urow
-                    nxt = (uh[:hi, hi : hi + BLOCK], ul[:hi, hi : hi + BLOCK])
-                    diag[...] = wb[kk + 1, kk + 1] - dot3(nxt, nxt, TN)
+                    xh[lo:hi, :lo], xl[lo:hi, :lo] = split(-dot3((ih, il), split(gx[:, :lo]), NN))
 
         return carry
 
@@ -388,10 +436,10 @@
     whole.wait()
 
     def spread(u, carry):
-        net.zslot(9 + 2 * u)
-        net.qslot(8 + 2 * u)
-        net.zslot(10 + 2 * u)
-        net.qslot(9 + 2 * u)
+        for n in range(AFTER):
+            slot = BEFORE + STEPS + EXTRA + AFTER * u + n - START
+            net.zslot(slot + 1)
+            net.qslot(slot)
         for m in range(4):
             pl.when(u > 0)(lambda: net.ztwin(m, 2 * u))
             net.ztwin(m, 2 * u + 1)
@@ -457,14 +505,15 @@
             pltpu.VMEM((STEPS, STEPS, BLOCK, BLOCK), f32),
             pltpu.VMEM(square, f32),
             pltpu.VMEM((STEPS, WIDTH, BLOCK), f32),
-            *(pltpu.VMEM(square, bf16) for _ in range(4)),
+            *(pltpu.VMEM(square, bf16) for _ in range(2)),
+            pltpu.VMEM((BLOCK, WIDTH), f32),
             *(pltpu.VMEM((ROUNDS, WIDE, WIDTH), bf16) for _ in range(2)),
             *(pltpu.VMEM((ROUNDS, WIDTH, WIDE), bf16) for _ in range(2)),
             pltpu.VMEM((BLOCK, BLOCK), f32),
             dma((3 + CHUNKS,)), dma,
             dma((STEPS, CHUNKS)), dma((2, 3, 4)),
-            dma((STEPS, CHUNKS)), dma((4, STEPS)),
-            dma((STEPS, STEPS)), dma((7, STEPS)),
+            dma((STEPS, CHUNKS)), dma((2, 4, STEPS)),
+            dma((STEPS, STEPS)), dma((5, 18)), dma((14, 2)),
         ],
         compiler_params=pltpu.CompilerParams(collective_id=0, has_side_effects=True, vmem_limit_bytes=58 << 20),
     )(blocked)

time: 135 us -> 117 us (0.87)
  the two profiles are of different devices: /device:TPU:16 before, /device:TPU:2 now
where the time goes in v3:
time: 117 us
  Pallas kernels  112 us (96%)
  local copies, waits for them, and re-layouts  4.79 us (4%)
    pallas_call x1, Pallas kernels, per_device(): pl.pallas_call(kernel, name='factor', out_shape=jax.ShapeDtypeStruct(squa...  112 us
    unnamed x1, local copies, waits for them, and re-layouts  4.79 us

profile of v3, /device:TPU:2, one launch (start us, length us, event | category | flops | bytes accessed | tf_op | source)
XLA Modules:
  0.0 116.6 jit_solution(8352758725145978350)
XLA Ops:
  0.0 111.8 %factor.1 = f32[1024,1024]{1,0:T(8,128)} custom-call(f32[1024,1024]{1,0:T(8,128)} %t_ref.1), custom_call_target="tpu_custom_call" | custom-call | tf_op jit(solution)/shard_map/factor/pallas_call | solution.py:496
  111.8 4.8 %copy.3 = f32[1024,1024]{1,0:T(8,128)} copy(f32[1024,1024]{1,0:T(8,128)} %factor.1) | data formatting | bytes 8388608

commit v4 on v3

--- a/solution.py
+++ b/solution.py
@@ -18,9 +18,11 @@
 STAGGER = 1
 BEFORE = 5
 EXTRA = 2
-START = 3
-AFTER = 0
+START = 2
+AFTER = 1
 PASS = (1, 2, 4)
+LAST_W = 11
+SKEW = 2
 WIDE = 2 * BLOCK
 ROUNDS = WIDTH // WIDE
 
@@ -114,7 +116,7 @@
 
     def zslot(self, slot):
         for m in range(4):
-            t = slot - self.zhops[m]
+            t = slot - SKEW * self.zhops[m]
 
             @pl.when((t >= 1) & (t < CHUNKS))
             def _():
@@ -129,7 +131,7 @@
 
     def qslot(self, slot):
         for i in range(STEPS):
-            t = slot - self.qhops[i]
+            t = slot - SKEW * self.qhops[i]
 
             @pl.when((t >= 0) & (t < CHUNKS))
             def _():
@@ -329,7 +331,7 @@
     return one(a[0], b[0]) + one(a[0], b[1]) + one(a[1], b[0])
 
 
-def kernel(t_ref, out, ap, aq, wb, tv, lpf, xh, xl, gx, lph, lpl, lqh, lql, diag, lsem, osem, *sems):
+def kernel(t_ref, out, ap, aq, wb, tv, lpf, xh, xl, gx, colh, coll, lph, lpl, lqh, lql, diag, lsem, osem, *sems):
     net = Links(ap, aq, wb, *sems)
     p, q = net.p, net.q
     barrier = pltpu.get_barrier_semaphore()
@@ -356,6 +358,16 @@
             row.start()
 
     whole.start()
+    xh[...] = jnp.zeros_like(xh)
+    xl[...] = jnp.zeros_like(xl)
+    gx[...] = jnp.zeros_like(gx)
+    colh[...] = jnp.zeros_like(colh)
+    coll[...] = jnp.zeros_like(coll)
+
+    for k in range(1, STEPS):
+        for j in range(k):
+            wb[k, j] = jnp.zeros((BLOCK, BLOCK), jnp.float32)
+
     pl.semaphore_wait(barrier, 14)
 
     @pl.when(q < STEPS)
@@ -367,9 +379,6 @@
     def _():
         for row in rows:
             row.wait()
-
-    xh[...] = jnp.zeros_like(xh)
-    xl[...] = jnp.zeros_like(xl)
 
     net.fsource()
 
@@ -397,42 +406,49 @@
         def _():
             wb[k, net.c] = ap[net.c, 0:BLOCK]
 
-    def step(k, carry):
+    def step(known, k, carry):
         def catch_up(slot, carry):
-            net.wslot(slot)
-            net.zslot(slot - START + 1)
-            net.qslot(slot - START)
+            pl.when(slot < LAST_W)(lambda: net.wslot(slot))
+
+            @pl.when((slot >= START) & (slot < START + CHUNKS + 5 * SKEW))
+            def _():
+                net.zslot(slot - START + 1)
+                net.qslot(slot - START)
+
             return carry
 
         lax.fori_loop(BEFORE + k + jnp.minimum(k, EXTRA), BEFORE + k + 1 + jnp.minimum(k + 1, EXTRA), catch_up, 0)
-        net.wtwin(k)
-        for kk in range(STEPS):
-            lo, hi = kk * BLOCK, (kk + 1) * BLOCK
-
-            @pl.when(k == kk)
-            def _():
-                if kk:
-                    x = (xh[:lo, :lo], xl[:lo, :lo])
-                    col = split(dot3(x, split(wb[0:kk, kk].reshape(lo, BLOCK)), NN))
-                    diag[...] = wb[kk, kk] - dot3(col, col, TN)
-                    gx[:, :lo] = dot3(col, x, TN)
-                else:
-                    diag[...] = wb[0, 0]
-
-        ih, il = split(invert_factor(diag[...]))
-        for kk in range(STEPS):
-            lo, hi = kk * BLOCK, (kk + 1) * BLOCK
-
-            @pl.when(k == kk)
-            def _():
-                xh[lo:hi, lo:hi] = ih
-                xl[lo:hi, lo:hi] = il
-                if kk:
-                    xh[lo:hi, :lo], xl[lo:hi, :lo] = split(-dot3((ih, il), split(gx[:, :lo]), NN))
-
+
+        @pl.when(k == 0)
+        def _():
+            net.wtwin(0)
+            diag[...] = wb[0, 0]
+
+        if known:
+            net.wtwin(k + 1)
+            full = slice(0, known)
+            x = (xh[full, full], xl[full, full])
+            part = split(dot3(x, split(wb[0 : known // BLOCK, k + 1].reshape(known, BLOCK)), NN))
+            cross = dot3((colh[full], coll[full]), part, TN)
+            square = dot3(part, part, TN)
+            across = dot3(part, x, TN)
+        inv = split(invert_factor(diag[...]))
+        mine = pl.ds(pl.multiple_of(k * BLOCK, BLOCK), BLOCK)
+        row = split(-dot3(inv, split(gx[...]), NN))
+        xh[mine, :], xl[mine, :] = row
+        xh[mine, mine], xl[mine, mine] = inv
+        if known:
+            last = split(dot3(inv, split(wb[k, k + 1] - cross), NN))
+            diag[...] = wb[k + 1, k + 1] - square - dot3(last, last, TN)
+            colh[full], coll[full] = part
+            colh[mine], coll[mine] = last
+            gx[...] = dot3(last, (xh[mine, :], xl[mine, :]), TN)
+            gx[:, full] = gx[:, full] + across
         return carry
 
-    lax.fori_loop(0, STEPS, step, 0)
+    lax.fori_loop(0, 5, functools.partial(step, 4 * BLOCK), 0)
+    lax.fori_loop(5, 7, functools.partial(step, 6 * BLOCK), 0)
+    step(0, jnp.int32(7), 0)
     whole.wait()
 
     def spread(u, carry):
@@ -507,6 +523,7 @@
             pltpu.VMEM((STEPS, WIDTH, BLOCK), f32),
             *(pltpu.VMEM(square, bf16) for _ in range(2)),
             pltpu.VMEM((BLOCK, WIDTH), f32),
+            *(pltpu.VMEM((WIDTH, BLOCK), bf16) for _ in range(2)),
             *(pltpu.VMEM((ROUNDS, WIDE, WIDTH), bf16) for _ in range(2)),
             *(pltpu.VMEM((ROUNDS, WIDTH, WIDE), bf16) for _ in range(2)),
             pltpu.VMEM((BLOCK, BLOCK), f32),

time: 117 us -> 110 us (0.940); the launches traced: 117 us -> 108 us
  Pallas kernels: 112 us -> 103 us
    pallas_call x1, Pallas kernels: 112 us -> 103 us  [per_device(): pl.pallas_call(kernel, name='factor', out_shape=jax.ShapeDtypeStruct(squa...]
where the time goes in v4:
time: 110 us; the launch traced here: 108 us
  Pallas kernels  103 us (94%)
  local copies, waits for them, and re-layouts  4.79 us (4%)
    pallas_call x1, Pallas kernels, per_device(): pl.pallas_call(kernel, name='factor', out_shape=jax.ShapeDtypeStruct(squa...  103 us
    unnamed x1, local copies, waits for them, and re-layouts  4.79 us

profile of v4, /device:TPU:2, one launch (start us, length us, event | category | flops | bytes accessed | tf_op | source)
XLA Modules:
  0.0 108.2 jit_solution(14988087279546014249)
XLA Ops:
  0.0 103.4 %factor.1 = f32[1024,1024]{1,0:T(8,128)} custom-call(f32[1024,1024]{1,0:T(8,128)} %t_ref.1), custom_call_target="tpu_custom_call" | custom-call | tf_op jit(solution)/shard_map/factor/pallas_call | solution.py:512
  103.4 4.8 %copy.3 = f32[1024,1024]{1,0:T(8,128)} copy(f32[1024,1024]{1,0:T(8,128)} %factor.1) | data formatting | bytes 8388608

commit v5 on v4

--- a/solution.py
+++ b/solution.py
@@ -311,8 +311,9 @@
         for j in range(TILE):
             rest = rest - lines[j] * times(row_of(r, j), left)
             brest = brest - lines[j] * times(row_of(b, j), left)
-        head, rest = rest[:TILE], rest[TILE:]
-        bhead, brest = brest[:TILE], brest[TILE:]
+        head, bhead = rest[:TILE], brest[:TILE]
+        if left > 1:
+            rest, brest = rest[TILE:], brest[TILE:]
     return jnp.concatenate(done, axis=0)
 
 
@@ -331,8 +332,19 @@
     return one(a[0], b[0]) + one(a[0], b[1]) + one(a[1], b[0])
 
 
-def kernel(t_ref, out, ap, aq, wb, tv, lpf, xh, xl, gx, colh, coll, lph, lpl, lqh, lql, diag, lsem, osem, *sems):
-    net = Links(ap, aq, wb, *sems)
+def kernel(t_ref, out, ap, aq, wb, tv, lpf, xh, xl, gx, colh, coll, lph, lpl, lqh, lql, diag, lsem, osem, zsem, qsem, wsem):
+    dma = pltpu.SemaphoreType.DMA
+    pl.run_scoped(
+        functools.partial(steps, t_ref, out, ap, aq, wb, tv, lpf, xh, xl, gx, colh, coll, lph, lpl, lqh, lql, diag, lsem, osem, zsem, qsem, wsem),
+        dma((2, 3, 4)), dma((2, 4, STEPS)), dma((5, 18)), dma((14, 2)),
+    )
+
+
+def steps(
+    t_ref, out, ap, aq, wb, tv, lpf, xh, xl, gx, colh, coll, lph, lpl, lqh, lql, diag, lsem, osem, zsem, qsem, wsem,
+    zsend, qsend, wsend, fsend,
+):
+    net = Links(ap, aq, wb, zsem, zsend, qsem, qsend, wsem, wsend, fsend)
     p, q = net.p, net.q
     barrier = pltpu.get_barrier_semaphore()
     for device in net.neighbours():
@@ -528,9 +540,7 @@
             *(pltpu.VMEM((ROUNDS, WIDTH, WIDE), bf16) for _ in range(2)),
             pltpu.VMEM((BLOCK, BLOCK), f32),
             dma((3 + CHUNKS,)), dma,
-            dma((STEPS, CHUNKS)), dma((2, 3, 4)),
-            dma((STEPS, CHUNKS)), dma((2, 4, STEPS)),
-            dma((STEPS, STEPS)), dma((5, 18)), dma((14, 2)),
+            dma((STEPS, CHUNKS)), dma((STEPS, CHUNKS)), dma((STEPS, STEPS)),
         ],
         compiler_params=pltpu.CompilerParams(collective_id=0, has_side_effects=True, vmem_limit_bytes=58 << 20),
     )(blocked)

time: 110 us -> 108 us (0.982)
    pallas_call x1, Pallas kernels: 103 us -> 102 us  [per_device(): pl.pallas_call(kernel, name='factor', out_shape=jax.ShapeDtypeStruct(squa...]
where the time goes in v5:
time: 108 us; the launch traced here: 106 us
  Pallas kernels  102 us (94%)
  local copies, waits for them, and re-layouts  4.79 us (4%)
    pallas_call x1, Pallas kernels, per_device(): pl.pallas_call(kernel, name='factor', out_shape=jax.ShapeDtypeStruct(squa...  102 us
    unnamed x1, local copies, waits for them, and re-layouts  4.79 us

profile of v5, /device:TPU:2, one launch (start us, length us, event | category | flops | bytes accessed | tf_op | source)
XLA Modules:
  0.0 106.4 jit_solution(5562975986463555979)
XLA Ops:
  0.0 101.6 %factor.1 = f32[1024,1024]{1,0:T(8,128)} custom-call(f32[1024,1024]{1,0:T(8,128)} %t_ref.1), custom_call_target="tpu_custom_call" | custom-call | tf_op jit(solution)/shard_map/factor/pallas_call | solution.py:524
  101.6 4.8 %copy.3 = f32[1024,1024]{1,0:T(8,128)} copy(f32[1024,1024]{1,0:T(8,128)} %factor.1) | data formatting | bytes 8388608

commit v6 on v5

--- a/solution.py
+++ b/solution.py
@@ -18,7 +18,7 @@
 STAGGER = 1
 BEFORE = 5
 EXTRA = 2
-START = 2
+START = 1
 AFTER = 1
 PASS = (1, 2, 4)
 LAST_W = 11

time: 108 us -> 108 us (level); the launches traced: 106 us -> 108 us
    pallas_call x1, Pallas kernels: 102 us -> 103 us  [per_device(): pl.pallas_call(kernel, name='factor', out_shape=jax.ShapeDtypeStruct(squa...]
where the time goes in v6:
time: 108 us
  Pallas kernels  103 us (95%)
  local copies, waits for them, and re-layouts  4.79 us (4%)
    pallas_call x1, Pallas kernels, per_device(): pl.pallas_call(kernel, name='factor', out_shape=jax.ShapeDtypeStruct(squa...  103 us
    unnamed x1, local copies, waits for them, and re-layouts  4.79 us

profile of v6, /device:TPU:2, one launch (start us, length us, event | category | flops | bytes accessed | tf_op | source)
XLA Modules:
  0.0 107.9 jit_solution(7555677249015955568)
XLA Ops:
  0.0 103.1 %factor.1 = f32[1024,1024]{1,0:T(8,128)} custom-call(f32[1024,1024]{1,0:T(8,128)} %t_ref.1), custom_call_target="tpu_custom_call" | custom-call | tf_op jit(solution)/shard_map/factor/pallas_call | solution.py:524
  103.1 4.8 %copy.3 = f32[1024,1024]{1,0:T(8,128)} copy(f32[1024,1024]{1,0:T(8,128)} %factor.1) | data formatting | bytes 8388608
